TPU v7x, 32 devices: a whole 2x2x4 slice. The times are simulated.
32 devices in a mesh: gx: 4 (over y, core), gy: 8 (over z, x).
Axes of the slice: x: 2, y: 2, z: 4, core: 2. Of those that a mesh axis runs over, the one named last changes fastest.
Arguments:
- old_master: float32 [32, 128, 1536], P('gx', 'gy'), may hold values from -3 to 3
- old_first: float32 [32, 128, 1536], P('gx', 'gy'), may hold values from -3 to 3
- old_second: float32 [32, 128, 1536], P('gx', 'gy'), may hold values from 0.01 to 1
- new_grad: bfloat16 [32, 128, 1536], P(('gx', 'gy')), may hold values from -3072 to 3072
- counts: int32 [32, 32], P(None, ('gx', 'gy')), may hold values from 1 to 72, as said below
- old_owner: int32 [32], replicated, may hold values from 0 to 31, each once
- new_owner: int32 [32], replicated, may hold values from 0 to 31, each once
Outputs:
- new_master: float32 [32, 128, 1536], P(('gx', 'gy'))
- new_first: float32 [32, 128, 1536], P(('gx', 'gy'))
- new_second: float32 [32, 128, 1536], P(('gx', 'gy'))
Inputs may be any that keep to these rules, and one draw needn't show every extreme that they name: `old_owner`: every number of 0 to 31 appears once. `new_owner`: every number of 0 to 31 appears once. `counts`: every device routed at least one token to every expert.
All inputs are finite; a program needn't handle non-finite values.
Results may differ from a plain program's by a relative error of at most 0.0003.
Values sent between devices are 32-bit elements; how exact they have to be, the bound alone decides.
A program may use at most 64 MiB of HBM per device.

v0:
```python
import jax
import jax.numpy as jnp
from jax import lax
from jax.sharding import PartitionSpec as P

first_correction = 1.0 - 0.9**10
second_correction = 1.0 - 0.999**10


def adam_step(master, first, second, grad, slot_count):
    scaled = grad.astype(jnp.float32) / slot_count
    new_first = 0.9 * first + 0.1 * scaled
    new_second = 0.999 * second + 0.001 * scaled * scaled
    step_dir = new_first / first_correction / (jnp.sqrt(new_second / second_correction) + 1e-08)
    new_master = master - 0.01 * (step_dir + 0.1 * master)
    return (new_master, new_first, new_second)


def reorder(block, groups_x, groups_y):
    total_rows = block.shape[1]
    piece = total_rows // (groups_x * groups_y)
    shaped = block.reshape(1, groups_x, groups_y, piece, block.shape[2])
    return shaped.transpose(0, 2, 1, 3, 4).reshape(1, total_rows, block.shape[2])


def body(old_master, old_first, old_second, new_grad, counts, old_owner, new_owner):
    experts = old_owner.shape[0]
    groups_x = lax.axis_size("gx")
    groups_y = lax.axis_size("gy")
    my_slot = lax.axis_index("gx") * groups_y + lax.axis_index("gy")
    slots = jnp.arange(experts, dtype=jnp.int32)
    onehot = new_owner[:, None] == slots[None, :]
    source = jnp.sum(jnp.where(onehot, old_owner[:, None], 0), axis=0)
    local_counts = counts[:, 0].astype(jnp.float32)
    by_rows = (
        lax.all_to_all(old_master, "gx", split_axis=1, concat_axis=0, tiled=True),
        lax.all_to_all(old_first, "gx", split_axis=1, concat_axis=0, tiled=True),
        lax.all_to_all(old_second, "gx", split_axis=1, concat_axis=0, tiled=True),
    )
    permuted = tuple((jnp.take(state, source, axis=0) for state in by_rows))
    landed = lax.all_to_all(permuted, ("gx", "gy"), split_axis=0, concat_axis=1, tiled=True)
    arrived = tuple((reorder(state, groups_x, groups_y) for state in landed))
    totals = lax.psum(local_counts, ("gx", "gy"))
    slot_count = jnp.sum(jnp.where(new_owner == my_slot, totals, jnp.float32(0.0)))
    return adam_step(arrived[0], arrived[1], arrived[2], new_grad, slot_count)


def solution(mesh):
    placed = (
        P("gx", "gy", None),
        P("gx", "gy", None),
        P("gx", "gy", None),
        P(("gx", "gy"), None, None),
        P(None, ("gx", "gy")),
        P(),
        P(),
    )
    return jax.shard_map(
        body,
        mesh=mesh,
        in_specs=placed,
        out_specs=(
            P(("gx", "gy"), None, None),
            P(("gx", "gy"), None, None),
            P(("gx", "gy"), None, None),
        ),
        check_vma=False,
    )
```

profile of v0, /device:TPU:0, one launch (start us, length us, event | category | flops | bytes accessed | tf_op | source)
XLA Modules:
  0.0 156.1 jit_solution(17211418162359433335)
XLA Ops:
  0.6 2.5 %copy.67 = f32[8,16,1536]{2,0,1:T(8,128)} copy(f32[8,16,1536]{2,1,0:T(8,128)} %param.9) | data formatting | bytes 1572864 | tf_op args[0]
  3.1 0.0 copy-start
  3.1 4.4 %all-to-all-start = ((f32[8,16,1536]{2,0,1:T(8,128)}), f32[8,16,1536]{2,0,1:T(8,128)S(1)}, u32[]{:S(2)}, u32[]{:S(2)}) async-start(f32[8,16,1536]{2,0,1:T(8,128)} %copy.67), calls=%async_computation | async-start | bytes 1572864 | tf_op jit(solution)/shard_map/all_to_all | solution.py:36
  7.5 0.0 copy-done
  7.5 1.3 copy.72
  8.8 0.0 copy-start.1
  8.8 10.3 %all-to-all-done = f32[8,16,1536]{2,0,1:T(8,128)S(1)} async-done(((f32[8,16,1536]{2,0,1:T(8,128)}), f32[8,16,1536]{2,0,1:T(8,128)S(1)}, u32[]{:S(2)}, u32[]{:S(2)}) %all-to-all-start) | async-done | bytes 786464 | tf_op jit(solution)/shard_map/all_to_all | solution.py:36
  19.1 3.5 %all-to-all-start.2 = ((f32[8,16,1536]{2,0,1:T(8,128)}), f32[8,16,1536]{2,0,1:T(8,128)S(1)}, u32[]{:S(2)}, u32[]{:S(2)}) async-start(f32[8,16,1536]{2,0,1:T(8,128)} %copy.72), calls=%async_computation.2 | async-start | bytes 1572864 | tf_op jit(solution)/shard_map/all_to_all | solution.py:37
  22.6 0.0 copy-done.1
  22.6 1.3 copy.78
  24.0 0.0 copy-start.3
  24.0 0.0 copy-start.4
  24.0 10.2 %all-to-all-done.2 = f32[8,16,1536]{2,0,1:T(8,128)S(1)} async-done(((f32[8,16,1536]{2,0,1:T(8,128)}), f32[8,16,1536]{2,0,1:T(8,128)S(1)}, u32[]{:S(2)}, u32[]{:S(2)}) %all-to-all-start.2) | async-done | bytes 786464 | tf_op jit(solution)/shard_map/all_to_all | solution.py:37
  34.2 3.5 %all-to-all-start.4 = ((f32[8,16,1536]{2,0,1:T(8,128)}), f32[8,16,1536]{2,0,1:T(8,128)S(1)}, u32[]{:S(2)}, u32[]{:S(2)}) async-start(f32[8,16,1536]{2,0,1:T(8,128)} %copy.78), calls=%async_computation.4 | async-start | bytes 1572864 | tf_op jit(solution)/shard_map/all_to_all | solution.py:38
  37.7 0.0 copy-done.3
  37.7 0.0 copy-done.4
  37.7 0.1 select_reduce_fusion
  37.9 0.1 copy.104
  37.9 0.5 copy.69
  38.4 0.1 copy.102
  38.5 1.4 copy.74
  39.9 1.0 gather_fusion
  40.9 2.2 %gather_fusion.1 = f32[32,4,1536]{2,1,0:T(4,128)S(1)} fusion(f32[32,4,1536]{2,1,0:T(4,128)} %copy.74, s32[1024]{0:T(1024)S(1)} %pad_clamp_fusion), kind=kCustom, calls=%fused_computation.1.clone | custom fusion | bytes 1572992 | tf_op jit(solution)/shard_map/jit(_take)/gather | solution.py:40
  43.1 6.2 %all-to-all-done.4 = f32[8,16,1536]{2,0,1:T(8,128)S(1)} async-done(((f32[8,16,1536]{2,0,1:T(8,128)}), f32[8,16,1536]{2,0,1:T(8,128)S(1)}, u32[]{:S(2)}, u32[]{:S(2)}) %all-to-all-start.4) | async-done | bytes 786464 | tf_op jit(solution)/shard_map/all_to_all | solution.py:38
  49.3 0.1 copy.101
  49.4 0.5 copy.80
  49.9 1.0 gather_fusion.2
  50.9 1.5 broadcast_select_fusion
  52.4 27.2 %all_to_all.81 = f32[32,4,1536]{2,1,0:T(4,128)S(1)} all-to-all(f32[32,4,1536]{2,1,0:T(4,128)S(1)} %get-tuple-element.13), channel_id=1, replica_groups=mesh['gx'=4,'gy'=8] {'gx','gy'}, dimensions={0} | all-to-all | bytes 1572864 | tf_op jit(solution)/shard_map/all_to_all | solution.py:41
  79.6 24.0 %all_to_all.82 = f32[32,4,1536]{2,1,0:T(4,128)S(1)} all-to-all(f32[32,4,1536]{2,1,0:T(4,128)S(1)} %get-tuple-element.14), channel_id=1, replica_groups=mesh['gx'=4,'gy'=8] {'gx','gy'}, dimensions={0} | all-to-all | bytes 1572864 | tf_op jit(solution)/shard_map/all_to_all | solution.py:41
  103.6 0.0 copy-start.5
  103.6 2.8 %all-to-all-start.1 = ((f32[32,4,1536]{2,1,0:T(4,128)}), f32[32,4,1536]{2,1,0:T(4,128)S(1)}, u32[]{:S(2)}, u32[]{:S(2)}) async-start(f32[32,4,1536]{2,1,0:T(4,128)} %get-tuple-element.15), calls=%async_computation.1 | async-start | bytes 1572864 | tf_op jit(solution)/shard_map/all_to_all | solution.py:41
  106.4 0.0 copy-done.5
  106.4 43.1 %psum.7 = f32[32]{0:T(128)S(1)} all-reduce(f32[32]{0:T(128)S(1)} %convert_bitcast_fusion), channel_id=1, replica_groups=mesh['gx'=4,'gy'=8] {'gx','gy'}, use_global_device_ids=true, to_apply=%region_1.3 | all-reduce | flops 32 | bytes 256 | tf_op jit(solution)/shard_map/psum | solution.py:43
  149.5 0.7 fusion.3
  150.2 0.3 fusion.1
  150.5 0.8 copy.82
  151.3 0.3 fusion.2
  151.6 0.8 copy.76
  152.4 0.0 all-to-all-done.1
  152.4 0.3 copy.103
  152.7 0.0 copy-start.2
  152.7 0.8 copy.71
  153.5 0.2 copy-done.2
  153.7 2.5 %multiply_subtract_fusion = (f32[1,128,1536]{2,1,0:T(8,128)}, f32[1,128,1536]{2,1,0:T(8,128)}, f32[1,128,1536]{2,1,0:T(8,128)}) fusion(f32[1,128,1536]{2,0,1:T(1,128)S(1)} %bitcast.45, f32[]{:T(128)} %fusion.3, bf16[1,128,1536]{2,1,0:T(8,128)(2,1)S(1)} %copy-done.2, f32[1,128,1536]{2,0,1:T(1,128)S(1)} %bitcast.44, f32[1,128,1536]{2,0,1:T(1,128)S(1)} %bitcast.43), kind=kLoop, calls=%fused_computation.14 | loop fusion | flops 2949120 | bytes 5111812 | tf_op jit(solution)/shard_map/sub | solution.py:15
  (4 shorter events, 0.0 us)
Async XLA Ops:
  3.1 4.4 %copy-start = (f32[8,16,1536]{2,1,0:T(8,128)S(1)}, f32[8,16,1536]{2,1,0:T(8,128)}, u32[]{:S(2)}) copy-start(f32[8,16,1536]{2,1,0:T(8,128)} %param.10) | copy-start | bytes 2359300
  3.1 16.0 %all-to-all-start = ((f32[8,16,1536]{2,0,1:T(8,128)}), f32[8,16,1536]{2,0,1:T(8,128)S(1)}, u32[]{:S(2)}, u32[]{:S(2)}) async-start(f32[8,16,1536]{2,0,1:T(8,128)} %copy.67), calls=%async_computation | async-start | bytes 1572864 | tf_op jit(solution)/shard_map/all_to_all | solution.py:36
  8.8 13.8 %copy-start.1 = (f32[8,16,1536]{2,1,0:T(8,128)S(1)}, f32[8,16,1536]{2,1,0:T(8,128)}, u32[]{:S(2)}) copy-start(f32[8,16,1536]{2,1,0:T(8,128)} %param.11) | copy-start | bytes 2359300
  19.1 15.1 %all-to-all-start.2 = ((f32[8,16,1536]{2,0,1:T(8,128)}), f32[8,16,1536]{2,0,1:T(8,128)S(1)}, u32[]{:S(2)}, u32[]{:S(2)}) async-start(f32[8,16,1536]{2,0,1:T(8,128)} %copy.72), calls=%async_computation.2 | async-start | bytes 1572864 | tf_op jit(solution)/shard_map/all_to_all | solution.py:37
  24.0 13.7 %copy-start.3 = (s32[32]{0:T(128)S(1)}, s32[32]{0:T(128)}, u32[]{:S(2)}) copy-start(s32[32]{0:T(128)} %param.15) | copy-start | bytes 388
  24.0 13.8 %copy-start.4 = (s32[32]{0:T(128)S(1)}, s32[32]{0:T(128)}, u32[]{:S(2)}) copy-start(s32[32]{0:T(128)} %param.14) | copy-start | bytes 388
  34.2 15.1 %all-to-all-start.4 = ((f32[8,16,1536]{2,0,1:T(8,128)}), f32[8,16,1536]{2,0,1:T(8,128)S(1)}, u32[]{:S(2)}, u32[]{:S(2)}) async-start(f32[8,16,1536]{2,0,1:T(8,128)} %copy.78), calls=%async_computation.4 | async-start | bytes 1572864 | tf_op jit(solution)/shard_map/all_to_all | solution.py:38
  103.6 2.8 %copy-start.5 = (s32[32,1]{0,1:T(1,128)S(1)}, s32[32,1]{0,1:T(1,128)}, u32[]{:S(2)}) copy-start(s32[32,1]{0,1:T(1,128)} %param.13) | copy-start | bytes 388
  103.6 48.8 %all-to-all-start.1 = ((f32[32,4,1536]{2,1,0:T(4,128)}), f32[32,4,1536]{2,1,0:T(4,128)S(1)}, u32[]{:S(2)}, u32[]{:S(2)}) async-start(f32[32,4,1536]{2,1,0:T(4,128)} %get-tuple-element.15), calls=%async_computation.1 | async-start | bytes 1572864 | tf_op jit(solution)/shard_map/all_to_all | solution.py:41
  152.7 1.0 copy-start.2
where the time goes:
time: 157 us; the launch traced here: 156 us
  blocking collectives  94.3 us (60%)
  waiting for transfers between devices  26.7 us (17%)
  local copies, waits for them, and re-layouts  14.8 us (9%)
  starting transfers between devices  14.1 us (9%)
  other arithmetic  5.31 us (3%)
    all_to_all x2, blocking collectives, body(): lax.all_to_all(permuted, ('gx', 'gy'), split_axis=0, concat_axis=1, tiled...  51.2 us
    psum x1, blocking collectives, body(): totals = lax.psum(local_counts, ('gx', 'gy'))  43.1 us
    all_to_all x1, waiting for transfers between devices, body(): lax.all_to_all(old_master, 'gx', split_axis=1, concat_axis=0, tiled=True)  10.3 us
    all_to_all x1, waiting for transfers between devices, body(): lax.all_to_all(old_first, 'gx', split_axis=1, concat_axis=0, tiled=True)  10.2 us
    all_to_all x1, waiting for transfers between devices, body(): lax.all_to_all(old_second, 'gx', split_axis=1, concat_axis=0, tiled=True)  6.23 us
    unnamed x15, local copies, waits for them, and re-layouts  5.34 us
    all_to_all x1, starting transfers between devices, body(): lax.all_to_all(old_master, 'gx', split_axis=1, concat_axis=0, tiled=True)  4.4 us
    gather x3, local copies, waits for them, and re-layouts, body(): permuted = tuple((jnp.take(state, source, axis=0) for state in by_rows))  4.19 us
  transfers between devices with their start and end apart: 4, of which 3 were waited for; matrix products, arithmetic and copies ran while one was open for 7% of the time, Pallas kernels for 0%

commit v1 on v0

--- a/solution.py
+++ b/solution.py
@@ -5,6 +5,28 @@
 
 first_correction = 1.0 - 0.9**10
 second_correction = 1.0 - 0.999**10
+
+
+def split_up(shard, dim, count):
+    before, after = (shard.shape[:dim], shard.shape[dim + 1 :])
+    return jnp.moveaxis(shard.reshape(*before, count, -1, *after), dim, 0)
+
+
+def in_order(blocks, dim):
+    blocks = jnp.moveaxis(blocks, 0, dim)
+    shape = blocks.shape
+    return blocks.reshape(*shape[:dim], shape[dim] * shape[dim + 1], *shape[dim + 2 :])
+
+
+def exchange_in_pairs(value, axis, split_dim, concat_dim):
+    size, index = (lax.axis_size(axis), lax.axis_index(axis))
+    parts = split_up(value, split_dim, size)
+    outs = [parts[index]]
+    for step in range(1, size):
+        sent = parts[index ^ step]
+        outs.append(lax.ppermute(sent, axis, [(i, i ^ step) for i in range(size)]))
+    parts = jnp.stack(outs)[index ^ jnp.arange(size)]
+    return in_order(parts, concat_dim)
 
 
 def adam_step(master, first, second, grad, slot_count):
@@ -35,7 +57,7 @@
     by_rows = (
         lax.all_to_all(old_master, "gx", split_axis=1, concat_axis=0, tiled=True),
         lax.all_to_all(old_first, "gx", split_axis=1, concat_axis=0, tiled=True),
-        lax.all_to_all(old_second, "gx", split_axis=1, concat_axis=0, tiled=True),
+        exchange_in_pairs(old_second, "gx", 1, 0),
     )
     permuted = tuple((jnp.take(state, source, axis=0) for state in by_rows))
     landed = lax.all_to_all(permuted, ("gx", "gy"), split_axis=0, concat_axis=1, tiled=True)

time: 157 us -> 143 us (0.911)
  waiting for transfers between devices: 26.7 us -> 15.9 us
  local copies, waits for them, and re-layouts: 14.8 us -> 12.2 us
    all_to_all x1, waiting for transfers between devices: 10.2 us -> 2.9 us  [body(): lax.all_to_all(old_first, 'gx', split_axis=1, concat_axis=0, tiled=True)]
    all_to_all x1 -> x0, waiting for transfers between devices: 6.23 us -> none  [body(): lax.all_to_all(old_second, 'gx', split_axis=1, concat_axis=0, tiled=True)]
    ppermute x0 -> x3, waiting for transfers between devices: none -> 4.88 us  [exchange_in_pairs(): outs.append(lax.ppermute(sent, axis, [(i, i ^ step) for i in range(size)]))]
    all_to_all x1 -> x0, starting transfers between devices: 3.49 us -> none  [body(): lax.all_to_all(old_second, 'gx', split_axis=1, concat_axis=0, tiled=True)]
    ppermute x0 -> x3, starting transfers between devices: none -> 2.44 us  [exchange_in_pairs(): outs.append(lax.ppermute(sent, axis, [(i, i ^ step) for i in range(size)]))]
    all_to_all x1, waiting for transfers between devices: 10.3 us -> 8.15 us  [body(): lax.all_to_all(old_master, 'gx', split_axis=1, concat_axis=0, tiled=True)]
    unnamed x15 -> x14, local copies, waits for them, and re-layouts: 5.34 us -> 4 us
  transfers between devices with their start and end apart: 4 -> 6, of which waited for: 3 -> 3; matrix products, arithmetic and copies ran while one was open for 7% -> 7% of each run, Pallas kernels for 0% -> 0%
where the time goes in v1:
time: 143 us
  blocking collectives  94.3 us (66%)
  waiting for transfers between devices  15.9 us (11%)
  starting transfers between devices  13.1 us (9%)
  local copies, waits for them, and re-layouts  12.2 us (9%)
  other arithmetic  6.41 us (4%)
    all_to_all x2, blocking collectives, body(): lax.all_to_all(permuted, ('gx', 'gy'), split_axis=0, concat_axis=1, tiled...  51.2 us
    psum x1, blocking collectives, body(): totals = lax.psum(local_counts, ('gx', 'gy'))  43.1 us
    all_to_all x1, waiting for transfers between devices, body(): lax.all_to_all(old_master, 'gx', split_axis=1, concat_axis=0, tiled=True)  8.15 us
    ppermute x3, waiting for transfers between devices, exchange_in_pairs(): outs.append(lax.ppermute(sent, axis, [(i, i ^ step) for i in range(size)]))  4.88 us
    all_to_all x1, starting transfers between devices, body(): lax.all_to_all(old_master, 'gx', split_axis=1, concat_axis=0, tiled=True)  4.4 us
    unnamed x14, local copies, waits for them, and re-layouts  4 us
    all_to_all x1, starting transfers between devices, body(): lax.all_to_all(old_first, 'gx', split_axis=1, concat_axis=0, tiled=True)  3.49 us
    gather x3, local copies, waits for them, and re-layouts, body(): permuted = tuple((jnp.take(state, source, axis=0) for state in by_rows))  3.05 us
  transfers between devices with their start and end apart: 6, of which 3 were waited for; matrix products, arithmetic and copies ran while one was open for 7% of the time, Pallas kernels for 0%

profile of v1, /device:TPU:0, one launch (start us, length us, event | category | flops | bytes accessed | tf_op | source)
XLA Modules:
  0.0 142.8 jit_solution(3876921758351770140)
XLA Ops:
  0.6 2.5 %copy.58 = f32[8,16,1536]{2,0,1:T(8,128)} copy(f32[8,16,1536]{2,1,0:T(8,128)} %param.9) | data formatting | bytes 1572864 | tf_op args[0]
  3.1 0.0 copy-start
  3.1 4.4 %all-to-all-start = ((f32[8,16,1536]{2,0,1:T(8,128)}), f32[8,16,1536]{2,0,1:T(8,128)S(1)}, u32[]{:S(2)}, u32[]{:S(2)}) async-start(f32[8,16,1536]{2,0,1:T(8,128)} %copy.58), calls=%async_computation | async-start | bytes 1572864 | tf_op jit(solution)/shard_map/all_to_all | solution.py:58
  7.5 0.0 copy-done
  7.5 0.2 reshape.111
  7.7 0.0 copy-start.1
  7.8 0.1 dynamic-slice_bitcast_fusion.3
  7.8 1.8 %collective-permute-start.2 = (f32[8,4,1536]{2,1,0:T(4,128)S(1)}, f32[8,4,1536]{2,1,0:T(4,128)S(1)}, u32[]{:S(2)}, u32[]{:S(2)}) collective-permute-start(f32[8,4,1536]{2,1,0:T(4,128)S(1)} %get-tuple-element.14), channel_id=1, source_target_pairs={{0,24},{8,16},{16,8},{24,0},{1,25},{9,17},{17,9},{25,1},{2,26},{10... | collective-permute-start | bytes 589832 | tf_op jit(solution)/shard_map/ppermute | solution.py:27
  9.6 0.6 collective-permute-start.1
  10.2 0.0 copy-start.3
  10.2 0.0 collective-permute-start
  10.3 0.0 copy-done.1
  10.3 1.3 copy.63
  11.6 0.0 copy-done.3
  11.6 0.0 copy-done.4
  11.6 0.1 select_reduce_fusion
  11.7 8.1 %all-to-all-done = f32[8,16,1536]{2,0,1:T(8,128)S(1)} async-done(((f32[8,16,1536]{2,0,1:T(8,128)}), f32[8,16,1536]{2,0,1:T(8,128)S(1)}, u32[]{:S(2)}, u32[]{:S(2)}) %all-to-all-start) | async-done | bytes 786464 | tf_op jit(solution)/shard_map/all_to_all | solution.py:58
  19.9 3.5 %all-to-all-start.2 = ((f32[8,16,1536]{2,0,1:T(8,128)}), f32[8,16,1536]{2,0,1:T(8,128)S(1)}, u32[]{:S(2)}, u32[]{:S(2)}) async-start(f32[8,16,1536]{2,0,1:T(8,128)} %copy.63), calls=%async_computation.2 | async-start | bytes 1572864 | tf_op jit(solution)/shard_map/all_to_all | solution.py:59
  23.4 0.0 collective-permute-done.2
  23.4 4.9 %collective-permute-done.1 = f32[8,4,1536]{2,1,0:T(4,128)S(1)} collective-permute-done((f32[8,4,1536]{2,1,0:T(4,128)S(1)}, f32[8,4,1536]{2,1,0:T(4,128)S(1)}, u32[]{:S(2)}, u32[]{:S(2)}) %collective-permute-start.1) | collective-permute-done | bytes 196640 | tf_op jit(solution)/shard_map/ppermute | solution.py:27
  28.3 0.0 collective-permute-done
  28.3 1.1 pad_maximum_fusion
  29.4 1.0 gather_fusion
  30.4 1.0 gather_fusion.3
  31.5 0.1 copy.90
  31.5 0.5 copy.60
  32.0 1.0 gather_fusion.1
  33.1 2.9 %all-to-all-done.2 = f32[8,16,1536]{2,0,1:T(8,128)S(1)} async-done(((f32[8,16,1536]{2,0,1:T(8,128)}), f32[8,16,1536]{2,0,1:T(8,128)S(1)}, u32[]{:S(2)}, u32[]{:S(2)}) %all-to-all-start.2) | async-done | bytes 786464 | tf_op jit(solution)/shard_map/all_to_all | solution.py:59
  36.0 0.1 copy.88
  36.0 0.5 copy.65
  36.5 1.0 gather_fusion.2
  37.6 1.5 %broadcast_select_fusion = (f32[32,4,1536]{2,1,0:T(4,128)S(1)}, f32[32,4,1536]{2,1,0:T(4,128)S(1)}, f32[32,4,1536]{2,1,0:T(4,128)}) fusion(f32[32,4,1536]{2,1,0:T(4,128)S(1)} %gather_fusion.3, pred[32]{0:T(512)(128)(4,1)S(1)} %compare_and_fusion, f32[32,4,1536]{2,1,0:T(4,128)S(1)} %gather_fusion.2, f32[32,4,1536]{2,1,0:T(4,128)S(1)} %gather_fusion.1), kind=kLoop, calls=%fused_computation.17 | loop fusion | flops 589824 | bytes 4718624 | tf_op jit(solution)/shard_map/jit(_take)/select_n | solution.py:62
  39.1 27.2 %all_to_all.63 = f32[32,4,1536]{2,1,0:T(4,128)S(1)} all-to-all(f32[32,4,1536]{2,1,0:T(4,128)S(1)} %get-tuple-element.17), channel_id=1, replica_groups=mesh['gx'=4,'gy'=8] {'gx','gy'}, dimensions={0} | all-to-all | bytes 1572864 | tf_op jit(solution)/shard_map/all_to_all | solution.py:63
  66.3 24.0 %all_to_all.64 = f32[32,4,1536]{2,1,0:T(4,128)S(1)} all-to-all(f32[32,4,1536]{2,1,0:T(4,128)S(1)} %get-tuple-element.18), channel_id=1, replica_groups=mesh['gx'=4,'gy'=8] {'gx','gy'}, dimensions={0} | all-to-all | bytes 1572864 | tf_op jit(solution)/shard_map/all_to_all | solution.py:63
  90.3 2.8 %all-to-all-start.1 = ((f32[32,4,1536]{2,1,0:T(4,128)}), f32[32,4,1536]{2,1,0:T(4,128)S(1)}, u32[]{:S(2)}, u32[]{:S(2)}) async-start(f32[32,4,1536]{2,1,0:T(4,128)} %get-tuple-element.19), calls=%async_computation.1 | async-start | bytes 1572864 | tf_op jit(solution)/shard_map/all_to_all | solution.py:63
  93.1 0.0 copy-done.5
  93.1 43.1 %psum.7 = f32[32]{0:T(128)S(1)} all-reduce(f32[32]{0:T(128)S(1)} %convert_bitcast_fusion), channel_id=1, replica_groups=mesh['gx'=4,'gy'=8] {'gx','gy'}, use_global_device_ids=true, to_apply=%region_1.3 | all-reduce | flops 32 | bytes 256 | tf_op jit(solution)/shard_map/psum | solution.py:65
  136.2 0.7 fusion.3
  136.8 0.3 fusion.1
  137.1 0.8 copy.70
  137.9 0.3 fusion.2
  138.2 0.8 copy.67
  139.0 0.0 all-to-all-done.1
  139.0 0.3 copy.89
  139.3 0.0 copy-start.2
  139.3 0.8 copy.62
  140.1 0.2 copy-done.2
  140.3 2.4 %multiply_subtract_fusion = (f32[1,128,1536]{2,1,0:T(8,128)}, f32[1,128,1536]{2,1,0:T(8,128)}, f32[1,128,1536]{2,1,0:T(8,128)}) fusion(f32[1,128,1536]{2,0,1:T(1,128)S(1)} %bitcast.52, f32[]{:T(128)} %fusion.3, bf16[1,128,1536]{2,1,0:T(8,128)(2,1)S(1)} %copy-done.2, f32[1,128,1536]{2,0,1:T(1,128)S(1)} %bitcast.51, f32[1,128,1536]{2,0,1:T(1,128)S(1)} %bitcast.50), kind=kLoop, calls=%fused_computation.15 | loop fusion | flops 2949120 | bytes 5111812 | tf_op jit(solution)/shard_map/sub | solution.py:37
  (8 shorter events, 0.0 us)
Async XLA Ops:
  3.1 4.4 %copy-start = (f32[8,16,1536]{2,1,0:T(8,128)S(1)}, f32[8,16,1536]{2,1,0:T(8,128)}, u32[]{:S(2)}) copy-start(f32[8,16,1536]{2,1,0:T(8,128)} %param.11) | copy-start | bytes 2359300
  3.1 16.8 %all-to-all-start = ((f32[8,16,1536]{2,0,1:T(8,128)}), f32[8,16,1536]{2,0,1:T(8,128)S(1)}, u32[]{:S(2)}, u32[]{:S(2)}) async-start(f32[8,16,1536]{2,0,1:T(8,128)} %copy.58), calls=%async_computation | async-start | bytes 1572864 | tf_op jit(solution)/shard_map/all_to_all | solution.py:58
  7.7 2.5 %copy-start.1 = (f32[8,16,1536]{2,1,0:T(8,128)S(1)}, f32[8,16,1536]{2,1,0:T(8,128)}, u32[]{:S(2)}) copy-start(f32[8,16,1536]{2,1,0:T(8,128)} %param.10) | copy-start | bytes 2359300
  7.8 15.6 %collective-permute-start.2 = (f32[8,4,1536]{2,1,0:T(4,128)S(1)}, f32[8,4,1536]{2,1,0:T(4,128)S(1)}, u32[]{:S(2)}, u32[]{:S(2)}) collective-permute-start(f32[8,4,1536]{2,1,0:T(4,128)S(1)} %get-tuple-element.14), channel_id=1, source_target_pairs={{0,24},{8,16},{16,8},{24,0},{1,25},{9,17},{17,9},{25,1},{2,26},{10... | collective-permute-start | bytes 589832 | tf_op jit(solution)/shard_map/ppermute | solution.py:27
  9.6 18.7 %collective-permute-start.1 = (f32[8,4,1536]{2,1,0:T(4,128)S(1)}, f32[8,4,1536]{2,1,0:T(4,128)S(1)}, u32[]{:S(2)}, u32[]{:S(2)}) collective-permute-start(f32[8,4,1536]{2,1,0:T(4,128)S(1)} %get-tuple-element.15), channel_id=1, source_target_pairs={{0,16},{8,24},{16,0},{24,8},{1,17},{9,25},{17,1},{25,9},{2,18},{10... | collective-permute-start | bytes 589832 | tf_op jit(solution)/shard_map/ppermute | solution.py:27
  10.2 1.4 copy-start.3
  10.2 1.4 copy-start.4
  10.2 18.1 %collective-permute-start = (f32[8,4,1536]{2,1,0:T(4,128)S(1)}, f32[8,4,1536]{2,1,0:T(4,128)}, u32[]{:S(2)}, u32[]{:S(2)}) collective-permute-start(f32[8,4,1536]{2,1,0:T(4,128)S(1)} %get-tuple-element.16), channel_id=1, source_target_pairs={{0,8},{8,0},{16,24},{24,16},{1,9},{9,1},{17,25},{25,17},{2,10},{10... | collective-permute-start | bytes 589832 | tf_op jit(solution)/shard_map/ppermute | solution.py:27
  19.9 16.1 %all-to-all-start.2 = ((f32[8,16,1536]{2,0,1:T(8,128)}), f32[8,16,1536]{2,0,1:T(8,128)S(1)}, u32[]{:S(2)}, u32[]{:S(2)}) async-start(f32[8,16,1536]{2,0,1:T(8,128)} %copy.63), calls=%async_computation.2 | async-start | bytes 1572864 | tf_op jit(solution)/shard_map/all_to_all | solution.py:59
  90.3 2.8 %copy-start.5 = (s32[32,1]{0,1:T(1,128)S(1)}, s32[32,1]{0,1:T(1,128)}, u32[]{:S(2)}) copy-start(s32[32,1]{0,1:T(1,128)} %param.13) | copy-start | bytes 388
  90.3 48.7 %all-to-all-start.1 = ((f32[32,4,1536]{2,1,0:T(4,128)}), f32[32,4,1536]{2,1,0:T(4,128)S(1)}, u32[]{:S(2)}, u32[]{:S(2)}) async-start(f32[32,4,1536]{2,1,0:T(4,128)} %get-tuple-element.19), calls=%async_computation.1 | async-start | bytes 1572864 | tf_op jit(solution)/shard_map/all_to_all | solution.py:63
  139.3 1.0 copy-start.2
